TPU v7x, 32 devices: a whole 2x2x4 slice. The times are simulated.
32 devices in a mesh: seq: 8 (over z, x), fsdp: 4 (over y, core).
Axes of the slice: x: 2, y: 2, z: 4, core: 2. Of those that a mesh axis runs over, the one named last changes fastest.
Arguments:
- tokens: bfloat16 [4, 1024, 1536], P('fsdp', 'seq'), may hold values from -6 to 6
- in_weight: bfloat16 [1536, 6400], P('fsdp'), may hold values from -0.15625 to 0.15625
- step_weight: bfloat16 [1536, 48], P('fsdp'), may hold values from -0.15625 to 0.15625
- conv_kernel: bfloat16 [4, 3328], P(None, 'fsdp'), may hold values from -3 to 3
- conv_bias: bfloat16 [3328], P('fsdp'), may hold values from -3 to 3
- step_bias: bfloat16 [48], P('fsdp'), may hold values from -6 to -3
- log_decay: bfloat16 [48], P('fsdp'), may hold values from -7 to 1
- skip_gain: bfloat16 [48], P('fsdp'), may hold values from 0.5 to 1.5
- gate_gain: bfloat16 [3072], P('fsdp'), may hold values from 0.5 to 1.5
- norm_gain: bfloat16 [1536], P('fsdp'), may hold values from 0.5 to 1.5
- out_weight: bfloat16 [3072, 1536], P('fsdp'), may hold values from -0.109375 to 0.109375
- cotangent: bfloat16 [4, 1024, 1536], P('fsdp', 'seq'), may hold values from -6 to 6
Outputs:
- block_out: bfloat16 [4, 1024, 1536], P('fsdp', 'seq')
- input_grad: float32 [4, 1024, 1536], P('fsdp', 'seq')
- in_weight_grad: float32 [1536, 6400], P('fsdp')
- step_weight_grad: float32 [1536, 48], P('fsdp')
- conv_kernel_grad: float32 [4, 3328], P(None, 'fsdp')
- conv_bias_grad: float32 [3328], P('fsdp')
- step_bias_grad: float32 [48], P('fsdp')
- log_decay_grad: float32 [48], P('fsdp')
- skip_gain_grad: float32 [48], P('fsdp')
- gate_gain_grad: float32 [3072], P('fsdp')
- norm_gain_grad: float32 [1536], P('fsdp')
- out_weight_grad: float32 [3072, 1536], P('fsdp')
All inputs are finite; a program needn't handle non-finite values.
Results may differ from a plain program's by a relative error of at most 0.012.
The roundings to bfloat16 on the way count: a program that leaves them out, or rounds other values in their place, can miss the bound.
Values may be sent and summed in bfloat16 or wider, within the bound.
A program may use at most 320 MiB of HBM per device.

v0:
```python
import jax
import jax.numpy as jnp
from jax import lax
from jax.sharding import PartitionSpec as P

N = 128
BLOCK = 256
epsilon = 1e-05
bf16 = jnp.bfloat16
f32 = jnp.float32


def block_step(carried, pieces, decay_rate):
    x_blk, step_blk, b_blk, c_blk = pieces
    cumulative = jnp.cumsum(step_blk * decay_rate[None, :], axis=0).T
    positions = jnp.arange(step_blk.shape[0])
    triangle = positions[:, None] >= positions[None, :]
    log_gap = jnp.where(triangle[None], cumulative[:, :, None] - cumulative[:, None, :], -1e30)
    scores = jnp.dot(c_blk, b_blk.T)
    mixing = jnp.exp(log_gap) * scores[None] * step_blk.T[:, None, :]
    y_inside = jnp.einsum("hij,jhp->ihp", mixing, x_blk)
    y_carried = jnp.exp(cumulative).T[:, :, None] * jnp.einsum("in,hpn->ihp", c_blk, carried)
    weighting = jnp.exp(cumulative[:, -1:] - cumulative) * step_blk.T
    renewed = jnp.exp(cumulative[:, -1])[:, None, None] * carried + jnp.einsum(
        "hj,jhp,jn->hpn", weighting, x_blk, b_blk
    )
    return (renewed, y_inside + y_carried)


def ssd_scan(x_heads, step_size, decay_rate, b_conv, c_conv, carried):
    length = step_size.shape[0]
    extent = min(BLOCK, length)
    number = length // extent
    pieces = (
        x_heads.reshape((number, extent) + x_heads.shape[1:]),
        step_size.reshape((number, extent) + step_size.shape[1:]),
        b_conv.reshape(number, extent, -1),
        c_conv.reshape(number, extent, -1),
    )
    outs = []
    for k in range(number):
        carried, out = block_step(carried, tuple((p[k] for p in pieces)), decay_rate)
        outs.append(out)
    return jnp.concatenate(outs, 0).reshape(x_heads.shape)


def prepare(extended, raw_steps, conv_kernel, conv_offset, step_bias, log_rates):
    kernel_width = conv_kernel.shape[0]
    length = extended.shape[0] - kernel_width + 1
    summed = conv_offset[None, :] + sum(
        (
            conv_kernel[offset][None, :] * extended[offset : offset + length]
            for offset in range(kernel_width)
        )
    )
    active = jax.nn.silu(summed)
    split_at = active.shape[1] - 2 * N
    step_size = jax.nn.softplus(raw_steps + step_bias[None, :])
    return (
        active[:, :split_at],
        active[:, split_at : split_at + N],
        active[:, split_at + N :],
        step_size,
        -jnp.exp(log_rates),
    )


def mix_out(x_conv, b_conv, c_conv, step_size, decay_rate, gate_in, skip_part, carried):
    length, head_count = step_size.shape
    x_heads = x_conv.reshape(length, head_count, -1)
    result = (
        ssd_scan(x_heads, step_size, decay_rate, b_conv, c_conv, carried)
        + skip_part[None, :, None] * x_heads
    )
    return result.reshape(length, -1) * jax.nn.silu(gate_in)


def contract(left, right, left_dim, right_dim):
    return lax.dot_general(
        left, right, (((left_dim,), (right_dim,)), ((), ())), preferred_element_type=f32
    )


def shards(
    tokens,
    in_weight,
    step_weight,
    conv_kernel,
    conv_bias,
    step_bias,
    log_decay,
    skip_gain,
    gate_gain,
    norm_gain,
    out_weight,
    cotangent,
):
    seqs = lax.axis_size("seq")
    fs = lax.axis_size("fsdp")
    pos = lax.axis_index("seq")
    fpos = lax.axis_index("fsdp")
    heads = step_weight.shape[1]
    inner = out_weight.shape[0] * fs
    width = tokens.shape[-1]
    hg = heads // seqs
    cols = inner // seqs
    col = pos * cols
    KW, conv_l = conv_kernel.shape

    def sl(a, start, size, axis):
        return lax.dynamic_slice_in_dim(a, start, size, axis)

    w_part = jnp.concatenate(
        [
            sl(in_weight, col, cols, 1),
            sl(in_weight, inner + col, cols, 1),
            in_weight[:, 2 * inner :],
            sl(step_weight, pos * hg, hg, 1),
        ],
        axis=1,
    )
    w_g = lax.all_gather(w_part, "fsdp", axis=0, tiled=True)
    small = jnp.concatenate(
        [conv_kernel.reshape(-1), conv_bias, step_bias, log_decay, skip_gain, gate_gain, norm_gain]
    )
    small = lax.all_gather(small, "fsdp", axis=0, tiled=False).astype(f32)
    at = [0]

    def take(n):
        r = small[:, at[0] : at[0] + n]
        at[0] += n
        return r

    kernel_f = take(KW * conv_l).reshape(fs, KW, conv_l).transpose(1, 0, 2).reshape(KW, -1)
    bias_f = take(conv_l).reshape(-1)
    step_bias_f = take(heads // fs).reshape(-1)
    decay_f = take(heads // fs).reshape(-1)
    skip_f = take(heads // fs).reshape(-1)
    gate_f = sl(take(inner // fs).reshape(-1), col, cols, 0)
    norm_f = take(width // fs).reshape(-1)
    tok = lax.all_gather(tokens[0], "seq", axis=0, tiled=True)
    cot = lax.all_gather(cotangent[0], "seq", axis=0, tiled=True)
    w_out = lax.all_gather(out_weight, "fsdp", axis=0, tiled=True)
    w_out_g = sl(w_out, col, cols, 0)
    length = tok.shape[0]
    own = length // seqs
    resid = tok.astype(f32)
    scale_in = lax.rsqrt(jnp.mean(resid * resid, axis=-1, keepdims=True) + epsilon)
    hidden = (resid * scale_in * norm_f[None]).astype(bf16)
    proj = contract(hidden, w_g, 1, 0).astype(bf16).astype(f32)
    gate_in = proj[:, :cols]
    body = proj[:, cols : 2 * cols + 2 * N]
    raw = proj[:, 2 * cols + 2 * N :]
    my_kernel = jnp.concatenate([sl(kernel_f, col, cols, 1), kernel_f[:, inner:]], axis=1)
    my_bias = jnp.concatenate([sl(bias_f, col, cols, 0), bias_f[inner:]], axis=0)
    my_step_bias = sl(step_bias_f, pos * hg, hg, 0)
    my_decay = sl(decay_f, pos * hg, hg, 0)
    my_skip = sl(skip_f, pos * hg, hg, 0)
    extended = jnp.concatenate([jnp.zeros((KW - 1, cols + 2 * N), f32), body], axis=0)
    prepared, pull_prepare = jax.vjp(
        prepare, extended, raw, my_kernel, my_bias, my_step_bias, my_decay
    )
    x_conv, b_conv, c_conv, step_size, decay_rate = prepared
    start = jnp.zeros((hg, cols // hg, N), f32)
    gated_f, pull_mix = jax.vjp(
        mix_out, x_conv, b_conv, c_conv, step_size, decay_rate, gate_in, my_skip, start
    )
    gated_b = gated_f.astype(bf16)
    gated = gated_b.astype(f32)
    mixed_grad = contract(cot, w_out_g, 1, 1)
    g = mixed_grad * gate_f[None]
    stats = jnp.stack([jnp.sum(gated * gated, axis=1), jnp.sum(g * gated, axis=1)])
    stats = lax.psum(stats, "seq") / inner
    scale_out = lax.rsqrt(stats[0] + epsilon)[:, None]
    mixed_norm = (gated * scale_out * gate_f[None]).astype(bf16)
    gate_gain_grad = jnp.sum(mixed_grad * gated * scale_out, axis=0)
    gated_grad = (scale_out * g - scale_out**3 * gated * stats[1][:, None]).astype(bf16)
    mixed_all = lax.all_to_all(mixed_norm, "seq", split_axis=0, concat_axis=1, tiled=True)
    my_tok = tokens[0].astype(f32)
    block_out = (my_tok + contract(mixed_all, w_out, 1, 0)).astype(bf16)
    out_part = contract(mixed_norm, cot, 0, 0)
    x_grad, b_grad, c_grad, step_grad, rate_grad, gate_grad, skip_grad, _ = pull_mix(
        gated_grad.astype(f32)
    )
    ext_grad, raw_grad, kernel_grad, bias_grad, step_bias_grad, decay_grad = pull_prepare(
        (x_grad, b_grad, c_grad, step_grad, rate_grad)
    )
    proj_grad = jnp.concatenate([gate_grad, ext_grad[KW - 1 :], raw_grad], axis=1).astype(bf16)
    hid_part = contract(proj_grad, w_g, 1, 1)
    hidden_grad = lax.psum_scatter(
        hid_part.astype(bf16), "seq", scatter_dimension=0, tiled=True
    ).astype(f32)
    in_part = contract(hidden, proj_grad, 0, 0)
    in_red = lax.psum_scatter(in_part.astype(bf16), "fsdp", scatter_dimension=0, tiled=True)
    in_all = lax.all_gather(in_red, "seq", axis=0, tiled=False).astype(f32)
    in_grad = jnp.concatenate(
        [
            jnp.moveaxis(in_all[:, :, :cols], 0, 1).reshape(-1, inner),
            jnp.moveaxis(in_all[:, :, cols : 2 * cols], 0, 1).reshape(-1, inner),
            jnp.sum(in_all[:, :, 2 * cols : 2 * cols + 2 * N], axis=0),
        ],
        axis=1,
    )
    step_w_grad = jnp.moveaxis(in_all[:, :, 2 * cols + 2 * N :], 0, 1).reshape(-1, heads)
    out_red = lax.psum_scatter(out_part.astype(bf16), "fsdp", scatter_dimension=0, tiled=True)
    out_all = lax.all_gather(out_red, ("seq", "fsdp"), axis=0, tiled=True)
    out_rows = inner // fs
    out_grad = sl(out_all, fpos * out_rows, out_rows, 0).astype(f32)
    own_scale = lax.rsqrt(jnp.mean(my_tok * my_tok, axis=-1, keepdims=True) + epsilon)
    norm_gain_grad = jnp.sum(hidden_grad * my_tok * own_scale, axis=0)
    e = hidden_grad * norm_f[None]
    inner_mean = jnp.mean(e * my_tok, axis=-1, keepdims=True)
    input_grad = cotangent[0].astype(f32) + own_scale * e - own_scale**3 * my_tok * inner_mean

    def put(a, total, start, axis):
        shape = list(a.shape)
        shape[axis] = total
        idx = [0] * a.ndim
        idx[axis] = start
        return lax.dynamic_update_slice(jnp.zeros(shape, f32), a, tuple(idx))

    conv = inner + 2 * N
    kg = jnp.concatenate([put(kernel_grad[:, :cols], inner, col, 1), kernel_grad[:, cols:]], 1)
    bg = jnp.concatenate([put(bias_grad[:cols], inner, col, 0), bias_grad[cols:]], 0)
    packed = jnp.concatenate(
        [
            kg.reshape(-1),
            bg,
            put(step_bias_grad, heads, pos * hg, 0),
            put(decay_grad, heads, pos * hg, 0),
            put(skip_grad, heads, pos * hg, 0),
            put(gate_gain_grad, inner, col, 0),
            norm_gain_grad,
        ]
    )
    packed = lax.psum(packed, ("seq", "fsdp"))
    at[0] = 0

    def grab(n, size, rows=None):
        r = packed[at[0] : at[0] + n]
        at[0] += n
        if rows:
            return sl(r.reshape(rows, -1), fpos * size, size, 1)
        return sl(r, fpos * size, size, 0)

    kernel_out = grab(KW * conv, conv_l, KW)
    bias_out = grab(conv, conv_l)
    sb_out = grab(heads, heads // fs)
    ld_out = grab(heads, heads // fs)
    sk_out = grab(heads, heads // fs)
    gg_out = grab(inner, inner // fs)
    ng_out = grab(width, width // fs)
    return (
        block_out[None],
        input_grad[None],
        in_grad,
        step_w_grad,
        kernel_out,
        bias_out,
        sb_out,
        ld_out,
        sk_out,
        gg_out,
        ng_out,
        out_grad,
    )


def solution(mesh):
    row = P("fsdp", None)
    tok = P("fsdp", "seq", None)
    one = P("fsdp")
    return jax.shard_map(
        shards,
        mesh=mesh,
        in_specs=(tok, row, row, P(None, "fsdp"), one, one, one, one, one, one, row, tok),
        out_specs=(tok, tok, row, row, P(None, "fsdp"), one, one, one, one, one, one, row),
        check_vma=False,
    )
```

profile of v0, /device:TPU:0, one launch (start us, length us, event | category | flops | bytes accessed | tf_op | source)
XLA Modules:
  0.0 861.9 jit_solution(4475649698283908109)
XLA Ops:
  13.7 13.6 %all-reduce.34 = bf16[21392]{0:T(1024)(128)(2,1)S(1)} all-reduce(bf16[21392]{0:T(1024)(128)(2,1)S(1)} %dynamic-update-slice), channel_id=2, replica_groups=mesh['seq'=8,'fsdp'=4] {'fsdp'}, use_global_device_ids=true, to_apply=%add.34 | all-reduce | flops 21392 | bytes 85568
  30.7 42.3 %all-gather.17.cloned.1.call-done = bf16[1,1024,1536]{2,1,0:T(8,128)(2,1)} async-done(((bf16[1,128,1536]{2,1,0:T(8,128)(2,1)}), bf16[1,1024,1536]{2,1,0:T(8,128)(2,1)}) %all-gather.17.cloned.1.call-update) | async-done | bytes 3145744 | tf_op jit(solution)/shard_map/all_gather | solution.py:141
  75.8 28.8 %all-gather.11.cloned.1.call-done = bf16[1536,1030]{1,0:T(8,128)(2,1)} async-done(((bf16[384,1030]{1,0:T(8,128)(2,1)}), bf16[1536,1030]{1,0:T(8,128)(2,1)}) %all-gather.11.cloned.1.call-update) | async-done | bytes 3164176 | tf_op jit(solution)/shard_map/all_gather | solution.py:122
  104.6 5.9 fusion.3
  134.5 32.4 %all-gather.19.cloned.1.call-done = bf16[1,1024,1536]{2,1,0:T(8,128)(2,1)} async-done(((bf16[1,128,1536]{2,1,0:T(8,128)(2,1)}), bf16[1,1024,1536]{2,1,0:T(8,128)(2,1)}) %all-gather.19.cloned.1.call-update) | async-done | bytes 3145744 | tf_op jit(solution)/shard_map/all_gather | solution.py:142
  166.9 64.3 %all-gather.13.cloned.1.call-done = bf16[3072,1536]{1,0:T(8,128)(2,1)} async-done(((bf16[768,1536]{1,0:T(8,128)(2,1)}), bf16[3072,1536]{1,0:T(8,128)(2,1)}) %all-gather.13.cloned.1.call-update) | async-done | bytes 9437200 | tf_op jit(solution)/shard_map/all_gather | solution.py:143
  231.3 6.0 fusion.20
  237.9 22.3 %psum.14 = f32[2,1024]{1,0:T(2,128)} all-reduce(f32[2,1024]{1,0:T(2,128)} %pad_maximum_fusion.6), channel_id=1, replica_groups=mesh['seq'=8,'fsdp'=4] {'seq'}, use_global_device_ids=true, to_apply=%region_11.12 | all-reduce | flops 2048 | bytes 16384 | tf_op jit(solution)/shard_map/psum | solution.py:173
  294.6 6.8 fusion.118
  302.8 7.5 reduce-window.70
  313.3 8.2 reduce-window.76
  330.9 7.6 reduce-window.74
  340.1 15.3 %reduce-window.66 = f32[6,2,128]{2,1,0:T(2,128)S(1)} reduce-window(f32[6,2,128]{2,1,0:T(2,128)S(1)} %reshape.527, f32[]{:T(128)} %constant.35.clone.1), window={size=1x1x128 pad=0_0x0_0x0_127}, to_apply=%region_21.22 | reduce-window | flops 195072 | bytes 12292 | tf_op jit(solution)/shard_map/reduce-window.8
  373.8 8.0 multiply_reduce_fusion.2
  385.8 6.0 convolution_convert_fusion.2
  392.5 6.2 convolution_convert_fusion
  410.0 52.5 %reduce-scatter.6.cloned.1.call-done = bf16[128,1536]{1,0:T(8,128)(2,1)} async-done(((bf16[1024,1536]{1,0:T(8,128)(2,1)}), bf16[128,1536]{1,0:T(8,128)(2,1)}) %reduce-scatter.6.cloned.1.call-update) | async-done | bytes 393232 | tf_op jit(solution)/shard_map/reduce_scatter | solution.py:190
  464.6 40.5 %reduce-scatter.10.cloned.1.call-done = bf16[384,1030]{1,0:T(8,128)(2,1)} async-done(((bf16[1536,1030]{1,0:T(8,128)(2,1)}), bf16[384,1030]{1,0:T(8,128)(2,1)}) %reduce-scatter.10.cloned.1.call-update) | async-done | bytes 791056
  507.3 26.0 %reduce-scatter.8.cloned.1.call-done = bf16[96,1536]{1,0:T(8,128)(2,1)} async-done(((bf16[384,1536]{1,0:T(8,128)(2,1)}), bf16[96,1536]{1,0:T(8,128)(2,1)}) %reduce-scatter.8.cloned.1.call-update) | async-done | bytes 294928 | tf_op jit(solution)/shard_map/reduce_scatter | solution.py:205
  534.4 5.8 all-to-all-start
  540.1 20.4 %all-to-all-done = bf16[8,128,384]{1,2,0:T(8,128)(2,1)S(1)} async-done(((bf16[8,128,384]{1,2,0:T(8,128)(2,1)}), bf16[8,128,384]{1,2,0:T(8,128)(2,1)S(1)}, u32[]{:S(2)}, u32[]{:S(2)}) %all-to-all-start) | async-done | bytes 786464 | tf_op jit(solution)/shard_map/all_to_all | solution.py:178
  560.6 6.0 fusion.16
  567.8 95.1 %all-reduce.37.cloned.1.call-done = f32[21392]{0:T(1024)} async-done(((f32[21392]{0:T(1024)}), f32[21392]{0:T(1024)}) %all-reduce.37.cloned.1.call-update) | async-done | bytes 85584 | tf_op jit(solution)/shard_map/psum | solution.py:236
  671.3 96.4 %all-gather.21.cloned.1.call-done = bf16[3072,1030]{0,1:T(8,128)(2,1)} async-done(((bf16[384,1030]{0,1:T(8,128)(2,1)}), bf16[3072,1030]{0,1:T(8,128)(2,1)}) %all-gather.21.cloned.1.call-update) | async-done | bytes 6328336 | tf_op jit(solution)/shard_map/all_gather | solution.py:195
  767.7 9.0 %convert_element_type.81 = f32[3072,1030]{0,1:T(8,128)} convert(bf16[3072,1030]{0,1:T(8,128)(2,1)} %all-gather.21.cloned.1.call-done) | non-fusion elementwise | flops 3164160 | bytes 18984960 | tf_op jit(solution)/shard_map/convert_element_type | solution.py:195
  776.7 12.2 %copy.259 = f32[129,8,8,384]{3,2,1,0:T(8,128)} copy(f32[129,8,8,384]{3,1,2,0:T(8,128)} %bitcast.562) | data formatting | bytes 25362432
  799.7 8.1 slice_bitcast_fusion.2
  807.8 6.1 copy.197
  813.9 5.7 copy.261
  819.6 6.1 copy.196
  831.9 8.4 pad_maximum_fusion
  840.3 9.8 %all-gather.15.cloned.1.call-done = bf16[3072,1536]{1,0:T(8,128)(2,1)} async-done(((bf16[96,1536]{1,0:T(8,128)(2,1)}), bf16[3072,1536]{1,0:T(8,128)(2,1)}) %all-gather.15.cloned.1.call-update) | async-done | bytes 9437200 | tf_op jit(solution)/shard_map/all_gather | solution.py:206
  (570 shorter events, 155.2 us)
Async XLA Ops:
  7.2 65.8 %all-gather.17.cloned.1.call-start = ((), (), s32[]{:S(2)}) async-start(), calls=%async_computation.10 | async-start | bytes 3538944 | tf_op jit(solution)/shard_map/all_gather | solution.py:141
  7.9 96.7 %all-gather.11.cloned.1.call-start = ((), (), s32[]{:S(2)}) async-start(), calls=%async_computation.4 | async-start | bytes 4423680 | tf_op jit(solution)/shard_map/all_gather | solution.py:122
  10.5 156.5 %all-gather.19.cloned.1.call-start = ((), (), s32[]{:S(2)}) async-start(), calls=%async_computation.11 | async-start | bytes 3538944 | tf_op jit(solution)/shard_map/all_gather | solution.py:142
  11.2 220.1 %all-gather.13.cloned.1.call-start = ((), (), s32[]{:S(2)}) async-start(), calls=%async_computation.5 | async-start | bytes 11796480 | tf_op jit(solution)/shard_map/all_gather | solution.py:143
  11.8 450.7 %reduce-scatter.6.cloned.1.call-start = ((), (), s32[]{:S(2)}) async-start(), calls=%async_computation.6 | async-start | bytes 3538944 | tf_op jit(solution)/shard_map/reduce_scatter | solution.py:190
  27.6 77.0 %copy-start.64 = (f32[1536]{0:T(1024)}, f32[1536]{0:T(1024)S(1)}, u32[]{:S(2)}) copy-start(f32[1536]{0:T(1024)S(1)} %mul.709) | copy-start | bytes 18436
  29.2 86.2 %copy-start.143 = (f32[6]{0:T(128)}, f32[6]{0:T(128)S(1)}, u32[]{:S(2)}) copy-start(f32[6]{0:T(128)S(1)} %dynamic_slice.59) | copy-start | bytes 76
  29.3 46.5 %copy-start.139 = (f32[48]{0:T(128)}, f32[48]{0:T(128)S(1)}, u32[]{:S(2)}) copy-start(f32[48]{0:T(128)S(1)} %reshape.513) | copy-start | bytes 580
  30.0 80.8 %copy-start.83 = (f32[640]{0:T(1024)}, f32[640]{0:T(1024)S(1)}, u32[]{:S(2)}) copy-start(f32[640]{0:T(1024)S(1)} %get-tuple-element.58) | copy-start | bytes 7684
  30.0 80.8 %copy-start.85 = (f32[640]{0:T(1024)}, f32[640]{0:T(1024)S(1)}, u32[]{:S(2)}) copy-start(f32[640]{0:T(1024)S(1)} %get-tuple-element.59) | copy-start | bytes 7684
  30.1 85.5 %copy-start.127 = (f32[6]{0:T(128)}, f32[6]{0:T(128)S(1)}, u32[]{:S(2)}) copy-start(f32[6]{0:T(128)S(1)} %fusion.310) | copy-start | bytes 76
  73.1 31.6 %copy-start.22 = (bf16[1,1024,1536]{2,1,0:T(8,128)(2,1)S(1)}, bf16[1,1024,1536]{2,1,0:T(8,128)(2,1)}, u32[]{:S(2)}) copy-start(bf16[1,1024,1536]{2,1,0:T(8,128)(2,1)} %all-gather.17.cloned.1.call-done) | copy-start | bytes 9437188
  75.8 34.7 %copy-start.128 = (f32[1024]{0:T(1024)}, f32[1024]{0:T(1024)S(1)}, u32[]{:S(2)}) copy-start(f32[1024]{0:T(1024)S(1)} %add_rsqrt_fusion) | copy-start | bytes 12292
  125.7 7.4 copy-start.95
  237.3 28.9 %copy-start.35 = (bf16[1024,384]{0,1:T(8,128)(2,1)}, bf16[1024,384]{0,1:T(8,128)(2,1)S(1)}, u32[]{:S(2)}) copy-start(bf16[1024,384]{0,1:T(8,128)(2,1)S(1)} %get-tuple-element.65) | copy-start | bytes 2359300
  267.4 9.9 %copy-start.15 = (f32[256,384]{0,1:T(8,128)}, f32[256,384]{0,1:T(8,128)S(1)}, u32[]{:S(2)}) copy-start(f32[256,384]{0,1:T(8,128)S(1)} %get-tuple-element.84) | copy-start | bytes 1179652
  267.4 13.9 %copy-start.14 = (f32[256,384]{0,1:T(8,128)}, f32[256,384]{0,1:T(8,128)S(1)}, u32[]{:S(2)}) copy-start(f32[256,384]{0,1:T(8,128)S(1)} %get-tuple-element.81) | copy-start | bytes 1179652
  283.9 7.8 copy-start.96
  283.9 8.0 copy-start.123
  284.0 7.9 copy-start.125
  294.6 35.5 %copy-start.94 = (f32[256,6]{0,1:T(8,128)S(1)}, f32[256,6]{0,1:T(8,128)}, u32[]{:S(2)}) copy-start(f32[256,6]{0,1:T(8,128)} %multiply_reduce_fusion.17) | copy-start | bytes 18436
  294.6 44.8 %copy-start.63 = (f32[1,6,2,128]{3,2,1,0:T(2,128)S(1)}, f32[1,6,2,128]{3,2,1,0:T(2,128)}, u32[]{:S(2)}) copy-start(f32[1,6,2,128]{3,2,1,0:T(2,128)} %copy-done.62) | copy-start | bytes 18436
  294.6 44.8 %copy-start.89 = (f32[256,6]{0,1:T(8,128)S(1)}, f32[256,6]{0,1:T(8,128)}, u32[]{:S(2)}) copy-start(f32[256,6]{0,1:T(8,128)} %multiply_reduce_fusion.19) | copy-start | bytes 18436
  373.8 8.0 copy-start.84
  373.8 8.0 copy-start.86
  391.8 113.3 %reduce-scatter.10.cloned.1.call-start = ((), (), s32[]{:S(2)}) async-start(), calls=%async_computation.13 | async-start | bytes 4423680
  402.4 130.9 %reduce-scatter.8.cloned.1.call-start = ((), (), s32[]{:S(2)}) async-start(), calls=%async_computation.8 | async-start | bytes 1474560 | tf_op jit(solution)/shard_map/reduce_scatter | solution.py:205
  407.9 255.0 %all-reduce.37.cloned.1.call-start = ((), (), s32[]{:S(2)}) async-start(), calls=%async_computation.7 | async-start | bytes 172032 | tf_op jit(solution)/shard_map/psum | solution.py:236
  463.8 69.5 %copy-start.21 = (bf16[48,8,8,128]{3,2,1,0:T(8,128)(2,1)S(1)}, bf16[48,8,8,128]{3,2,1,0:T(8,128)(2,1)}, u32[]{:S(2)}) copy-start(bf16[48,8,8,128]{3,2,1,0:T(8,128)(2,1)} %get-tuple-element.85) | copy-start | bytes 2359300
  464.5 303.2 %all-gather.21.cloned.1.call-start = ((), (), s32[]{:S(2)}) async-start(), calls=%async_computation.12 | async-start | bytes 7133184 | tf_op jit(solution)/shard_map/all_gather | solution.py:195
  507.3 342.8 %all-gather.15.cloned.1.call-start = ((), (), s32[]{:S(2)}) async-start(), calls=%async_computation.9 | async-start | bytes 9732096 | tf_op jit(solution)/shard_map/all_gather | solution.py:206
  534.4 26.2 %all-to-all-start = ((bf16[8,128,384]{1,2,0:T(8,128)(2,1)}), bf16[8,128,384]{1,2,0:T(8,128)(2,1)S(1)}, u32[]{:S(2)}, u32[]{:S(2)}) async-start(bf16[8,128,384]{1,2,0:T(8,128)(2,1)} %bitcast.553), calls=%async_computation | async-start | bytes 1572864 | tf_op jit(solution)/shard_map/all_to_all | solution.py:178
  (131 other events, 382.5 us)
Sparse Core Ops, SparseCore 0:
  10.2 62.8 all-gather.16
  75.2 29.3 all-gather.10
  106.8 60.0 all-gather.18
  168.3 62.8 all-gather.12
  391.9 70.5 reduce-scatter.5
  465.5 39.5 reduce-scatter.9
  507.6 25.6 reduce-scatter.7
  539.4 123.3 all-reduce.36
  665.5 102.1 all-gather.20
  770.5 79.6 all-gather.14
where the time goes:
time: 870 us; the launch traced here: 862 us
  waiting for transfers between devices  511 us (59%)
  other arithmetic  116 us (13%)
  local copies, waits for them, and re-layouts  100 us (11%)
  matrix products  75.5 us (9%)
  blocking collectives  35.9 us (4%)
  between operations  17.3 us (2%)
    all_gather x1, waiting for transfers between devices, shards(): in_all = lax.all_gather(in_red, 'seq', axis=0, tiled=False).astype(f32)  96.4 us
    psum x1, waiting for transfers between devices, shards(): packed = lax.psum(packed, ('seq', 'fsdp'))  95.1 us
    all_gather x1, waiting for transfers between devices, shards(): w_out = lax.all_gather(out_weight, 'fsdp', axis=0, tiled=True)  64.3 us
    reduce_scatter x1, waiting for transfers between devices, shards(): lax.psum_scatter(hid_part.astype(bf16), 'seq', scatter_dimension=0, tiled...  52.5 us
    another operation x17, other arithmetic  49.7 us
    unnamed x11, waiting for transfers between devices  42.5 us
    all_gather x1, waiting for transfers between devices, shards(): tok = lax.all_gather(tokens[0], 'seq', axis=0, tiled=True)  42.3 us
    unnamed x312, local copies, waits for them, and re-layouts  41.4 us
  transfers between devices with their start and end apart: 11, of which 11 were waited for; matrix products, arithmetic and copies ran while one was open for 17% of the time, Pallas kernels for 0%

commit v1 on v0

--- a/solution.py
+++ b/solution.py
@@ -8,6 +8,17 @@
 epsilon = 1e-05
 bf16 = jnp.bfloat16
 f32 = jnp.float32
+
+
+def turned_line(x, mesh_axis, dim):
+    size = lax.axis_size(mesh_axis)
+    right = [(i, (i + 1) % size) for i in range(size)]
+    blocks = [x]
+    for far in range(1, size):
+        blocks = [lax.ppermute(blocks[0], mesh_axis, right), *blocks]
+    full = jnp.concatenate(blocks, axis=dim)
+    offset = (lax.axis_index(mesh_axis) + 1) * blocks[-1].shape[dim]
+    return jnp.roll(full, offset, axis=dim)
 
 
 def block_step(carried, pieces, decay_rate):
@@ -140,7 +151,7 @@
     norm_f = take(width // fs).reshape(-1)
     tok = lax.all_gather(tokens[0], "seq", axis=0, tiled=True)
     cot = lax.all_gather(cotangent[0], "seq", axis=0, tiled=True)
-    w_out = lax.all_gather(out_weight, "fsdp", axis=0, tiled=True)
+    w_out = turned_line(out_weight, "fsdp", 0)
     w_out_g = sl(w_out, col, cols, 0)
     length = tok.shape[0]
     own = length // seqs

time: 870 us -> 802 us (0.922)
  waiting for transfers between devices: 511 us -> 414 us
  local copies, waits for them, and re-layouts: 100 us -> 118 us
  blocking collectives: 35.9 us -> 53 us
  other arithmetic: 116 us -> 103 us
    all_gather x1 -> x0, waiting for transfers between devices: 64.3 us -> none  [shards(): w_out = lax.all_gather(out_weight, 'fsdp', axis=0, tiled=True)]
    all_gather x1, waiting for transfers between devices: 42.3 us -> 0.01 us  [shards(): tok = lax.all_gather(tokens[0], 'seq', axis=0, tiled=True)]
    ppermute x0 -> x3, waiting for transfers between devices: none -> 28.6 us  [turned_line(): blocks = [lax.ppermute(blocks[0], mesh_axis, right), *blocks]]
    all_gather x1, waiting for transfers between devices: 32.4 us -> 7.87 us  [shards(): cot = lax.all_gather(cotangent[0], 'seq', axis=0, tiled=True)]
    unnamed x312 -> x339, local copies, waits for them, and re-layouts: 41.4 us -> 62.4 us
    unnamed x1, blocking collectives: 13.6 us -> 32.6 us
    unnamed x11 -> x10, waiting for transfers between devices: 42.5 us -> 41.3 us
  transfers between devices with their start and end apart: 11 -> 13, of which waited for: 11 -> 10; matrix products, arithmetic and copies ran while one was open for 17% -> 21% of each run, Pallas kernels for 0% -> 0%
where the time goes in v1:
time: 802 us; the launch traced here: 795 us
  waiting for transfers between devices  414 us (52%)
  local copies, waits for them, and re-layouts  118 us (15%)
  other arithmetic  103 us (13%)
  matrix products  82.4 us (10%)
  blocking collectives  53 us (7%)
  between operations  17.3 us (2%)
    all_gather x1, waiting for transfers between devices, shards(): in_all = lax.all_gather(in_red, 'seq', axis=0, tiled=False).astype(f32)  96.4 us
    psum x1, waiting for transfers between devices, shards(): packed = lax.psum(packed, ('seq', 'fsdp'))  93.5 us
    unnamed x339, local copies, waits for them, and re-layouts  62.4 us
    reduce_scatter x1, waiting for transfers between devices, shards(): lax.psum_scatter(hid_part.astype(bf16), 'seq', scatter_dimension=0, tiled...  53.7 us
    another operation x17, other arithmetic  42.6 us
    unnamed x10, waiting for transfers between devices  41.3 us
    dot_general x6, matrix products, contract(): lax.dot_general(left, right, (((left_dim,), (right_dim,)), ((), ())), pre...  36.1 us
    all_gather x1, waiting for transfers between devices, shards(): w_g = lax.all_gather(w_part, 'fsdp', axis=0, tiled=True)  33.4 us
  transfers between devices with their start and end apart: 13, of which 10 were waited for; matrix products, arithmetic and copies ran while one was open for 21% of the time, Pallas kernels for 0%

profile of v1, /device:TPU:0, one launch (start us, length us, event | category | flops | bytes accessed | tf_op | source)
XLA Modules:
  0.0 794.8 jit_solution(13595292609054639683)
XLA Ops:
  11.2 28.6 %collective-permute-done = bf16[768,1536]{1,0:T(8,128)(2,1)} collective-permute-done((bf16[768,1536]{1,0:T(8,128)(2,1)S(1)}, bf16[768,1536]{1,0:T(8,128)(2,1)}, u32[]{:S(2)}, u32[]{:S(2)}) %collective-permute-start) | collective-permute-done | bytes 2359328 | tf_op jit(solution)/shard_map/ppermute | solution.py:18
  41.8 32.6 %all-reduce.34 = bf16[21392]{0:T(1024)(128)(2,1)S(1)} all-reduce(bf16[21392]{0:T(1024)(128)(2,1)S(1)} %dynamic-update-slice), channel_id=2, replica_groups=mesh['seq'=8,'fsdp'=4] {'fsdp'}, use_global_device_ids=true, to_apply=%add.34 | all-reduce | flops 21392 | bytes 85568
  80.8 33.4 %all-gather.10.cloned.1.call-done = bf16[1536,1030]{1,0:T(8,128)(2,1)} async-done(((bf16[384,1030]{1,0:T(8,128)(2,1)}), bf16[1536,1030]{1,0:T(8,128)(2,1)}) %all-gather.10.cloned.1.call-update) | async-done | bytes 3164176 | tf_op jit(solution)/shard_map/all_gather | solution.py:133
  114.3 5.9 fusion.5
  168.8 7.9 all-gather.16.cloned.1.call-done
  176.7 6.0 fusion.29
  183.4 20.4 %psum.14 = f32[2,1024]{1,0:T(2,128)} all-reduce(f32[2,1024]{1,0:T(2,128)} %pad_maximum_fusion.6), channel_id=1, replica_groups=mesh['seq'=8,'fsdp'=4] {'seq'}, use_global_device_ids=true, to_apply=%region_11.12 | all-reduce | flops 2048 | bytes 16384 | tf_op jit(solution)/shard_map/psum | solution.py:184
  204.5 5.3 multiply_reduce_fusion.4
  224.3 4.9 fusion.127
  231.1 8.8 %reduce-window.66 = f32[6,2,128]{2,1,0:T(2,128)} reduce-window(f32[6,2,128]{2,1,0:T(2,128)} %reshape.527, f32[]{:T(128)} %constant.91.clone.1), window={size=1x1x128 pad=0_0x0_0x0_127}, to_apply=%region_21.22 | reduce-window | flops 195072 | bytes 12292 | tf_op jit(solution)/shard_map/reduce-window.8
  258.8 7.6 reduce-window.74
  270.7 7.6 reduce-window.76
  278.6 7.7 reduce-window.70
  318.1 6.0 convolution_convert_fusion.2
  324.8 6.2 convolution_convert_fusion
  342.2 53.7 %reduce-scatter.6.cloned.1.call-done = bf16[128,1536]{1,0:T(8,128)(2,1)} async-done(((bf16[1024,1536]{1,0:T(8,128)(2,1)}), bf16[128,1536]{1,0:T(8,128)(2,1)}) %reduce-scatter.6.cloned.1.call-update) | async-done | bytes 393232 | tf_op jit(solution)/shard_map/reduce_scatter | solution.py:201
  397.9 40.5 %reduce-scatter.10.cloned.1.call-done = bf16[384,1030]{1,0:T(8,128)(2,1)} async-done(((bf16[1536,1030]{1,0:T(8,128)(2,1)}), bf16[384,1030]{1,0:T(8,128)(2,1)}) %reduce-scatter.10.cloned.1.call-update) | async-done | bytes 791056
  440.6 25.8 %reduce-scatter.8.cloned.1.call-done = bf16[96,1536]{1,0:T(8,128)(2,1)} async-done(((bf16[384,1536]{1,0:T(8,128)(2,1)}), bf16[96,1536]{1,0:T(8,128)(2,1)}) %reduce-scatter.8.cloned.1.call-update) | async-done | bytes 294928 | tf_op jit(solution)/shard_map/reduce_scatter | solution.py:216
  467.4 5.8 all-to-all-start
  473.2 20.4 %all-to-all-done = bf16[8,128,384]{1,2,0:T(8,128)(2,1)S(1)} async-done(((bf16[8,128,384]{1,2,0:T(8,128)(2,1)}), bf16[8,128,384]{1,2,0:T(8,128)(2,1)S(1)}, u32[]{:S(2)}, u32[]{:S(2)}) %all-to-all-start) | async-done | bytes 786464 | tf_op jit(solution)/shard_map/all_to_all | solution.py:189
  493.7 7.5 fusion.23
  502.4 93.5 %all-reduce.37.cloned.1.call-done = f32[21392]{0:T(1024)} async-done(((f32[21392]{0:T(1024)}), f32[21392]{0:T(1024)}) %all-reduce.37.cloned.1.call-update) | async-done | bytes 85584 | tf_op jit(solution)/shard_map/psum | solution.py:247
  604.3 96.4 %all-gather.18.cloned.1.call-done = bf16[3072,1030]{0,1:T(8,128)(2,1)} async-done(((bf16[384,1030]{0,1:T(8,128)(2,1)}), bf16[3072,1030]{0,1:T(8,128)(2,1)}) %all-gather.18.cloned.1.call-update) | async-done | bytes 6328336 | tf_op jit(solution)/shard_map/all_gather | solution.py:206
  700.7 9.0 %convert_element_type.81 = f32[3072,1030]{0,1:T(8,128)} convert(bf16[3072,1030]{0,1:T(8,128)(2,1)} %all-gather.18.cloned.1.call-done) | non-fusion elementwise | flops 3164160 | bytes 18984960 | tf_op jit(solution)/shard_map/convert_element_type | solution.py:206
  709.7 12.3 %copy.259 = f32[129,8,8,384]{3,2,1,0:T(8,128)} copy(f32[129,8,8,384]{3,1,2,0:T(8,128)} %bitcast.561) | data formatting | bytes 25362432
  722.0 5.2 slice_bitcast_fusion
  734.6 6.1 copy.196
  740.7 5.4 copy.260
  746.1 6.3 copy.197
  752.5 5.4 copy.261
  761.5 8.5 %pad_maximum_fusion = f32[384,6400]{1,0:T(8,128)} fusion(f32[384,256]{1,0:T(8,128)S(1)} %copy.198, f32[384,3072]{1,0:T(8,128)} %bitcast.566, f32[384,3072]{1,0:T(8,128)} %bitcast.565), kind=kLoop, calls=%fused_computation.1 | loop fusion | flops 4915200 | bytes 19660800 | tf_op jit(solution)/shard_map/concatenate | solution.py:207
  770.0 13.2 %all-gather.12.cloned.1.call-done = bf16[3072,1536]{1,0:T(8,128)(2,1)} async-done(((bf16[96,1536]{1,0:T(8,128)(2,1)}), bf16[3072,1536]{1,0:T(8,128)(2,1)}) %all-gather.12.cloned.1.call-update) | async-done | bytes 9437200 | tf_op jit(solution)/shard_map/all_gather | solution.py:217
  (602 shorter events, 173.6 us)
Async XLA Ops:
  7.2 70.8 %all-gather.14.cloned.1.call-start = ((), (), s32[]{:S(2)}) async-start(), calls=%async_computation.9 | async-start | bytes 3538944 | tf_op jit(solution)/shard_map/all_gather | solution.py:152
  7.9 106.3 %all-gather.10.cloned.1.call-start = ((), (), s32[]{:S(2)}) async-start(), calls=%async_computation.4 | async-start | bytes 4423680 | tf_op jit(solution)/shard_map/all_gather | solution.py:133
  8.2 31.7 %copy-start.137 = (bf16[4,832]{1,0:T(4,128)(2,1)S(1)}, bf16[4,832]{1,0:T(4,128)(2,1)}, u32[]{:S(2)}) copy-start(bf16[4,832]{1,0:T(4,128)(2,1)} %param.15) | copy-start | bytes 19972
  8.2 31.7 %copy-start.157 = (u32[32]{0:T(128)S(1)}, u32[32]{0:T(128)}, u32[]{:S(2)}) copy-start(u32[32]{0:T(128)} %constant.183) | copy-start | bytes 388
  8.2 33.0 %copy-start.148 = (bf16[832]{0:T(1024)(128)(2,1)S(1)}, bf16[832]{0:T(1024)(128)(2,1)}, u32[]{:S(2)}) copy-start(bf16[832]{0:T(1024)(128)(2,1)} %param.16) | copy-start | bytes 4996
  8.3 33.0 %copy-start.149 = (bf16[768]{0:T(1024)(128)(2,1)S(1)}, bf16[768]{0:T(1024)(128)(2,1)}, u32[]{:S(2)}) copy-start(bf16[768]{0:T(1024)(128)(2,1)} %param.20) | copy-start | bytes 4612
  8.3 33.0 %copy-start.152 = (bf16[384]{0:T(512)(128)(2,1)S(1)}, bf16[384]{0:T(512)(128)(2,1)}, u32[]{:S(2)}) copy-start(bf16[384]{0:T(512)(128)(2,1)} %param.21) | copy-start | bytes 2308
  8.3 33.0 %copy-start.153 = (bf16[12]{0:T(256)(128)(2,1)S(1)}, bf16[12]{0:T(256)(128)(2,1)}, u32[]{:S(2)}) copy-start(bf16[12]{0:T(256)(128)(2,1)} %param.17) | copy-start | bytes 76
  8.3 33.0 %copy-start.154 = (bf16[12]{0:T(256)(128)(2,1)S(1)}, bf16[12]{0:T(256)(128)(2,1)}, u32[]{:S(2)}) copy-start(bf16[12]{0:T(256)(128)(2,1)} %param.18) | copy-start | bytes 76
  8.3 33.0 %copy-start.155 = (bf16[12]{0:T(256)(128)(2,1)S(1)}, bf16[12]{0:T(256)(128)(2,1)}, u32[]{:S(2)}) copy-start(bf16[12]{0:T(256)(128)(2,1)} %param.19) | copy-start | bytes 76
  10.6 166.1 %all-gather.16.cloned.1.call-start = ((), (), s32[]{:S(2)}) async-start(), calls=%async_computation.10 | async-start | bytes 3538944 | tf_op jit(solution)/shard_map/all_gather | solution.py:153
  10.7 29.1 %collective-permute-start = (bf16[768,1536]{1,0:T(8,128)(2,1)S(1)}, bf16[768,1536]{1,0:T(8,128)(2,1)}, u32[]{:S(2)}, u32[]{:S(2)}) collective-permute-start(bf16[768,1536]{1,0:T(8,128)(2,1)S(1)} %copy-done.17), channel_id=1, source_target_pairs={{0,1},{1,2},{2,3},{3,0},{4,5},{5,6},{6,7},{7,4},{8,9},{9,10},{10,1... | collective-permute-start | bytes 7077896 | tf_op jit(solution)/shard_map/ppermute | solution.py:18
  39.8 38.0 %collective-permute-start.1 = (bf16[768,1536]{1,0:T(8,128)(2,1)}, bf16[768,1536]{1,0:T(8,128)(2,1)}, u32[]{:S(2)}, u32[]{:S(2)}) collective-permute-start(bf16[768,1536]{1,0:T(8,128)(2,1)} %collective-permute-done), channel_id=1, source_target_pairs={{0,1},{1,2},{2,3},{3,0},{4,5},{5,6},{6,7},{7,4},{8,9},{9,10},{10,1... | collective-permute-start | bytes 7077896 | tf_op jit(solution)/shard_map/ppermute | solution.py:18
  39.8 356.0 %reduce-scatter.6.cloned.1.call-start = ((), (), s32[]{:S(2)}) async-start(), calls=%async_computation.5 | async-start | bytes 3538944 | tf_op jit(solution)/shard_map/reduce_scatter | solution.py:201
  74.7 45.5 %copy-start.67 = (f32[1536]{0:T(1024)}, f32[1536]{0:T(1024)S(1)}, u32[]{:S(2)}) copy-start(f32[1536]{0:T(1024)S(1)} %mul.712) | copy-start | bytes 18436
  74.9 52.8 %copy-start.150 = (f32[6]{0:T(128)}, f32[6]{0:T(128)S(1)}, u32[]{:S(2)}) copy-start(f32[6]{0:T(128)S(1)} %dynamic_slice.66) | copy-start | bytes 76
  75.0 45.2 %copy-start.146 = (f32[48]{0:T(128)}, f32[48]{0:T(128)S(1)}, u32[]{:S(2)}) copy-start(f32[48]{0:T(128)S(1)} %reshape.513) | copy-start | bytes 580
  77.1 43.3 %copy-start.86 = (f32[640]{0:T(1024)}, f32[640]{0:T(1024)S(1)}, u32[]{:S(2)}) copy-start(f32[640]{0:T(1024)S(1)} %get-tuple-element.58) | copy-start | bytes 7684
  77.1 43.3 %copy-start.88 = (f32[640]{0:T(1024)}, f32[640]{0:T(1024)S(1)}, u32[]{:S(2)}) copy-start(f32[640]{0:T(1024)S(1)} %get-tuple-element.59) | copy-start | bytes 7684
  77.2 50.7 %copy-start.138 = (f32[6]{0:T(128)}, f32[6]{0:T(128)S(1)}, u32[]{:S(2)}) copy-start(f32[6]{0:T(128)S(1)} %fusion.320) | copy-start | bytes 76
  77.8 68.0 %collective-permute-start.2 = (bf16[768,1536]{1,0:T(8,128)(2,1)}, bf16[768,1536]{1,0:T(8,128)(2,1)}, u32[]{:S(2)}, u32[]{:S(2)}) collective-permute-start(bf16[768,1536]{1,0:T(8,128)(2,1)} %collective-permute-done.1), channel_id=1, source_target_pairs={{0,1},{1,2},{2,3},{3,0},{4,5},{5,6},{6,7},{7,4},{8,9},{9,10},{10,1... | collective-permute-start | bytes 7077896 | tf_op jit(solution)/shard_map/ppermute | solution.py:18
  78.0 36.3 %copy-start.26 = (bf16[1,1024,1536]{2,1,0:T(8,128)(2,1)S(1)}, bf16[1,1024,1536]{2,1,0:T(8,128)(2,1)}, u32[]{:S(2)}) copy-start(bf16[1,1024,1536]{2,1,0:T(8,128)(2,1)} %all-gather.14.cloned.1.call-done) | copy-start | bytes 9437188
  80.8 39.4 %copy-start.140 = (f32[1024]{0:T(1024)}, f32[1024]{0:T(1024)S(1)}, u32[]{:S(2)}) copy-start(f32[1024]{0:T(1024)S(1)} %add_rsqrt_fusion) | copy-start | bytes 12292
  182.7 27.1 %copy-start.42 = (bf16[1024,384]{0,1:T(8,128)(2,1)}, bf16[1024,384]{0,1:T(8,128)(2,1)S(1)}, u32[]{:S(2)}) copy-start(bf16[1024,384]{0,1:T(8,128)(2,1)S(1)} %get-tuple-element.65) | copy-start | bytes 2359300
  324.1 114.2 %reduce-scatter.10.cloned.1.call-start = ((), (), s32[]{:S(2)}) async-start(), calls=%async_computation.12 | async-start | bytes 4423680
  334.8 131.6 %reduce-scatter.8.cloned.1.call-start = ((), (), s32[]{:S(2)}) async-start(), calls=%async_computation.7 | async-start | bytes 1474560 | tf_op jit(solution)/shard_map/reduce_scatter | solution.py:216
  340.3 255.6 %all-reduce.37.cloned.1.call-start = ((), (), s32[]{:S(2)}) async-start(), calls=%async_computation.6 | async-start | bytes 172032 | tf_op jit(solution)/shard_map/psum | solution.py:247
  340.6 125.8 %copy-start.25 = (bf16[48,8,8,128]{3,2,1,0:T(8,128)(2,1)S(1)}, bf16[48,8,8,128]{3,2,1,0:T(8,128)(2,1)}, u32[]{:S(2)}) copy-start(bf16[48,8,8,128]{3,2,1,0:T(8,128)(2,1)} %get-tuple-element.85) | copy-start | bytes 2359300
  397.8 302.8 %all-gather.18.cloned.1.call-start = ((), (), s32[]{:S(2)}) async-start(), calls=%async_computation.11 | async-start | bytes 7133184 | tf_op jit(solution)/shard_map/all_gather | solution.py:206
  440.5 342.7 %all-gather.12.cloned.1.call-start = ((), (), s32[]{:S(2)}) async-start(), calls=%async_computation.8 | async-start | bytes 9732096 | tf_op jit(solution)/shard_map/all_gather | solution.py:217
  467.4 26.2 %all-to-all-start = ((bf16[8,128,384]{1,2,0:T(8,128)(2,1)}), bf16[8,128,384]{1,2,0:T(8,128)(2,1)S(1)}, u32[]{:S(2)}, u32[]{:S(2)}) async-start(bf16[8,128,384]{1,2,0:T(8,128)(2,1)} %bitcast.552), calls=%async_computation | async-start | bytes 1572864 | tf_op jit(solution)/shard_map/all_to_all | solution.py:189
  761.5 26.2 %copy-start.1 = (bf16[384,48]{0,1:T(8,128)(2,1)S(1)}, bf16[384,48]{0,1:T(8,128)(2,1)}, u32[]{:S(2)}) copy-start(bf16[384,48]{0,1:T(8,128)(2,1)} %param.14) | copy-start | bytes 110596
  (143 other events, 574.4 us)
Sparse Core Ops, SparseCore 0:
  10.2 62.7 all-gather.13
  75.1 39.0 all-gather.9
  116.4 60.1 all-gather.15
  324.3 71.5 reduce-scatter.5
  398.8 39.4 reduce-scatter.9
  440.8 25.5 reduce-scatter.7
  472.5 123.2 all-reduce.36
  598.5 102.1 all-gather.17
  703.6 79.6 all-gather.11
